TPU v7x, 128 devices: a whole 4x4x4 slice. The times are simulated.
128 devices in a mesh: dp: 16 (over x_hi, z, core), blk: 8 (over y, x_lo).
Axes of the slice: x: 4 (x_hi: 2, x_lo: 2; x = x_hi * 2 + x_lo), y: 4, z: 4, core: 2. Of those that a mesh axis runs over, the one named last changes fastest.
Arguments:
- inputs: bfloat16 [512, 8192], P('blk', 'dp'), may hold values from -6 to 6
- upstream: bfloat16 [512, 8192], P('blk', 'dp'), may hold values from -1.5 to 1.5
- gate_weight: bfloat16 [8192, 14784], P('dp', 'blk'), may hold values from -0.0625 to 0.0625
- up_weight: bfloat16 [8192, 14784], P('dp', 'blk'), may hold values from -0.0625 to 0.0625
- down_weight: bfloat16 [14784, 8192], P('blk', 'dp'), may hold values from -0.046875 to 0.046875
Outputs:
- input_grad: bfloat16 [512, 8192], P('blk', 'dp')
- gate_grad: bfloat16 [8192, 14784], P('dp', 'blk')
- up_grad: bfloat16 [8192, 14784], P('dp', 'blk')
- down_grad: bfloat16 [14784, 8192], P('blk', 'dp')
All inputs are finite; a program needn't handle non-finite values.
Results may differ from a plain program's by a relative error of at most 0.005.
Values may be sent and summed in bfloat16 or wider, within the bound.
A program may use at most 128 MiB of HBM per device.

v0:
```python
import jax
import jax.numpy as jnp
from jax import lax
from jax.sharding import PartitionSpec as P


def sent_together(arrays, axis, dim, along):
    both = jnp.concatenate(arrays, axis=along)
    filled, at, outs = (lax.all_gather(both, axis, axis=dim, tiled=True), 0, [])
    for a in arrays:
        outs.append(lax.slice_in_dim(filled, at, at + a.shape[along], axis=along))
        at += a.shape[along]
    return tuple(outs)


def in_blocks(array, dim, peers):
    shape = array.shape
    parts = array.reshape(*shape[:dim], peers, shape[dim] // peers, *shape[dim + 1 :])
    return jnp.moveaxis(parts, dim, 0)


def sent_and_summed(array, axis, dim):
    peers = lax.axis_size(axis)
    parts = lax.all_to_all(in_blocks(array, dim, peers), axis, 0, 0, tiled=True)
    return jnp.sum(parts, axis=0)


def contract_last(left, right):
    return lax.dot_general(
        left, right, (((1,), (1,)), ((), ())), preferred_element_type=jnp.float32
    )


def contract_first(left, right):
    return lax.dot_general(
        left, right, (((0,), (0,)), ((), ())), preferred_element_type=jnp.float32
    )


def elementwise(gate, up, back):
    sig = jax.nn.sigmoid(gate)
    hidden = (gate * sig * up).astype(jnp.bfloat16)
    up_delta = (back * gate * sig).astype(jnp.bfloat16)
    gate_delta = (back * up * sig * (1.0 + gate * (1.0 - sig))).astype(jnp.bfloat16)
    return (hidden, gate_delta, up_delta)


def local(inputs, upstream, gate_weight, up_weight, down_weight):
    rows_all, grads_all = sent_together((inputs, upstream), "blk", 0, 1)
    gate_part = jnp.dot(rows_all, gate_weight, preferred_element_type=jnp.float32)
    up_part = jnp.dot(rows_all, up_weight, preferred_element_type=jnp.float32)
    back_part = contract_last(grads_all, down_weight)
    gate, up, back = lax.psum((gate_part, up_part, back_part), "dp")
    hidden, gate_delta, up_delta = elementwise(gate, up, back)
    down_grad = contract_first(hidden, grads_all).astype(jnp.bfloat16)
    gate_grad = contract_first(rows_all, gate_delta).astype(jnp.bfloat16)
    up_grad = contract_first(rows_all, up_delta).astype(jnp.bfloat16)
    partial_input = contract_last(gate_delta, gate_weight) + contract_last(up_delta, up_weight)
    input_grad = sent_and_summed(partial_input, "blk", 0)
    return (input_grad.astype(jnp.bfloat16), gate_grad, up_grad, down_grad)


def solution(mesh):
    return jax.shard_map(
        local,
        mesh=mesh,
        in_specs=(P("blk", "dp"), P("blk", "dp"), P("dp", "blk"), P("dp", "blk"), P("blk", "dp")),
        out_specs=(P("blk", "dp"), P("dp", "blk"), P("dp", "blk"), P("blk", "dp")),
        check_vma=False,
    )
```

profile of v0, /device:TPU:1, one launch (start us, length us, event | category | flops | bytes accessed | tf_op | source)
XLA Modules:
  0.0 270.1 jit_solution(6070670908177451077)
XLA Ops:
  7.2 0.0 copy-start
  7.2 0.0 all-gather.2.cloned.1.call-start
  7.2 1.7 pad_maximum_fusion
  8.9 0.0 all-gather.2.cloned.1.call-update
  8.9 0.0 all-reduce.3.cloned.1.call-start
  9.0 39.6 %all-gather.2.cloned.1.call-done = bf16[512,1024]{1,0:T(8,128)(2,1)} async-done(((bf16[64,1024]{1,0:T(8,128)(2,1)}), bf16[512,1024]{1,0:T(8,128)(2,1)}) %all-gather.2.cloned.1.call-update) | async-done | bytes 1048592 | tf_op jit(solution)/shard_map/all_gather | solution.py:9
  48.6 4.3 %fusion.5 = f32[512,1848]{0,1:T(8,128)} fusion(bf16[512,1848]{0,1:T(8,128)(2,1)S(1)} %copy-done, bf16[512,1024]{1,0:T(8,128)(2,1)} %all-gather.2.cloned.1.call-done), kind=kOutput, calls=%fused_computation.13 | convolution fusion | flops 968884224 | bytes 6201344 | tf_op jit(solution)/shard_map/dot_general | solution.py:50
  52.9 3.1 %fusion.7 = f32[512,1848]{0,1:T(8,128)} fusion(bf16[512,1848]{0,1:T(8,128)(2,1)S(1)} %copy-done.1, bf16[512,1024]{1,0:T(8,128)(2,1)S(1)} %copy-done.8), kind=kOutput, calls=%fused_computation.15 | convolution fusion | flops 968884224 | bytes 6201344 | tf_op jit(solution)/shard_map/dot_general | solution.py:51
  56.0 3.1 %fusion.1 = f32[512,1848]{0,1:T(8,128)} fusion(bf16[1848,512]{1,0:T(8,128)(2,1)S(1)} %copy-done.10, bf16[512,1024]{1,0:T(8,128)(2,1)S(1)} %copy-done.8), kind=kOutput, calls=%fused_computation.9 | convolution fusion | flops 968884224 | bytes 6201344 | tf_op jit(solution)/shard_map/dot_general | solution.py:29
  59.1 0.0 all-reduce.3.cloned.1.call-update
  59.1 176.1 %all-reduce.3.cloned.1.call-done = (f32[512,1848]{0,1:T(8,128)}, f32[512,1848]{0,1:T(8,128)}, f32[512,1848]{0,1:T(8,128)}) async-done(((f32[512,1848]{0,1:T(8,128)}, f32[512,1848]{0,1:T(8,128)}, f32[512,1848]{0,1:T(8,128)}), (f32[512,1848]{0,1:T(8,128)}, f32[512,1848]{0,1:T(8,128)}, f32[512,1848]{0,1:T(8,128)})) %all-reduce.3.cloned.1.call-update) | async-done | bytes 11354128 | tf_op jit(solution)/shard_map/psum | solution.py:53
  235.2 5.2 %multiply_convert_fusion.1 = (bf16[512,1848]{0,1:T(8,128)(2,1)S(1)}, bf16[512,1848]{0,1:T(8,128)(2,1)S(1)}) fusion(f32[512,1848]{0,1:T(8,128)} %get-tuple-element.5, f32[512,1848]{0,1:T(8,128)} %get-tuple-element.4, f32[512,1848]{0,1:T(8,128)} %get-tuple-element.6), kind=kLoop, calls=%fused_computation.1 | loop fusion | flops 12300288 | bytes 15138816 | tf_op jit(solution)/shard_map/convert_element_type | solution.py:43
  240.4 0.0 copy-start.5
  240.4 0.0 copy-start.2
  240.4 1.3 fusion.10
  241.7 0.6 copy-done.3
  242.3 1.0 copy-done.2
  243.3 2.4 convolution_add_fusion
  245.7 4.0 %all-to-all-start = ((f32[8,64,512]{2,1,0:T(8,128)}), f32[8,64,512]{2,1,0:T(8,128)S(1)}, u32[]{:S(2)}, u32[]{:S(2)}) async-start(f32[8,64,512]{2,1,0:T(8,128)} %bitcast.10), calls=%async_computation | async-start | bytes 2097152 | tf_op jit(solution)/shard_map/all_to_all | solution.py:24
  249.7 4.2 %convolution_convert_fusion.2 = bf16[512,1848]{0,1:T(8,128)(2,1)} fusion(bf16[512,1848]{0,1:T(8,128)(2,1)} %copy-done.5, bf16[512,1024]{1,0:T(8,128)(2,1)} %all-gather.2.cloned.1.call-done), kind=kOutput, calls=%fused_computation.6 | convolution fusion | flops 969830400 | bytes 4308992 | tf_op jit(solution)/shard_map/dot_general | solution.py:35
  253.9 3.6 %convolution_convert_fusion.1 = bf16[512,1848]{0,1:T(8,128)(2,1)} fusion(bf16[512,1848]{0,1:T(8,128)(2,1)S(1)} %copy-done.4, bf16[512,1024]{1,0:T(8,128)(2,1)} %all-gather.2.cloned.1.call-done), kind=kOutput, calls=%fused_computation.5 | convolution fusion | flops 969830400 | bytes 4308992 | tf_op jit(solution)/shard_map/dot_general | solution.py:35
  257.5 2.6 convolution_convert_fusion
  260.1 2.4 all-to-all-done
  262.5 0.7 reduce_sum.9
  (17 shorter events, 0.0 us)
Async XLA Ops:
  7.2 41.4 %copy-start = (bf16[512,1848]{0,1:T(8,128)(2,1)S(1)}, bf16[512,1848]{0,1:T(8,128)(2,1)}, u32[]{:S(2)}) copy-start(bf16[512,1848]{0,1:T(8,128)(2,1)} %param.7) | copy-start | bytes 5677060
  7.2 41.4 %all-gather.2.cloned.1.call-start = ((), (), s32[]{:S(2)}) async-start(), calls=%async_computation.1 | async-start | bytes 1179648 | tf_op jit(solution)/shard_map/all_gather | solution.py:9
  8.9 226.3 %all-reduce.3.cloned.1.call-start = ((), (), s32[]{:S(2)}) async-start(), calls=%async_computation.2 | async-start | bytes 22708224 | tf_op jit(solution)/shard_map/psum | solution.py:53
  48.6 4.3 %copy-start.1 = (bf16[512,1848]{0,1:T(8,128)(2,1)S(1)}, bf16[512,1848]{0,1:T(8,128)(2,1)}, u32[]{:S(2)}) copy-start(bf16[512,1848]{0,1:T(8,128)(2,1)} %param.8) | copy-start | bytes 5677060
  48.6 4.3 %copy-start.8 = (bf16[512,1024]{1,0:T(8,128)(2,1)S(1)}, bf16[512,1024]{1,0:T(8,128)(2,1)}, u32[]{:S(2)}) copy-start(bf16[512,1024]{1,0:T(8,128)(2,1)} %all-gather.2.cloned.1.call-done) | copy-start | bytes 3145732
  52.9 3.1 %copy-start.10 = (bf16[1848,512]{1,0:T(8,128)(2,1)S(1)}, bf16[1848,512]{1,0:T(8,128)(2,1)}, u32[]{:S(2)}) copy-start(bf16[1848,512]{1,0:T(8,128)(2,1)} %param.9) | copy-start | bytes 5677060
  240.4 1.3 copy-start.5
  240.4 1.9 copy-start.3
  240.4 2.9 %copy-start.2 = (bf16[512,1848]{0,1:T(8,128)(2,1)S(1)}, bf16[512,1848]{0,1:T(8,128)(2,1)}, u32[]{:S(2)}) copy-start(bf16[512,1848]{0,1:T(8,128)(2,1)} %param.8) | copy-start | bytes 5677060
  245.7 16.9 %all-to-all-start = ((f32[8,64,512]{2,1,0:T(8,128)}), f32[8,64,512]{2,1,0:T(8,128)S(1)}, u32[]{:S(2)}, u32[]{:S(2)}) async-start(f32[8,64,512]{2,1,0:T(8,128)} %bitcast.10), calls=%async_computation | async-start | bytes 2097152 | tf_op jit(solution)/shard_map/all_to_all | solution.py:24
  249.7 4.2 %copy-start.4 = (bf16[512,1848]{0,1:T(8,128)(2,1)S(1)}, bf16[512,1848]{0,1:T(8,128)(2,1)}, u32[]{:S(2)}) copy-start(bf16[512,1848]{0,1:T(8,128)(2,1)} %copy-done.3) | copy-start | bytes 5677060
  249.7 7.8 %copy-start.7 = (f32[512,1848]{0,1:T(8,128)S(1)}, f32[512,1848]{0,1:T(8,128)}, u32[]{:S(2)}) copy-start(f32[512,1848]{0,1:T(8,128)} %get-tuple-element.6) | copy-start | bytes 11354116
  253.9 3.6 %copy-start.6 = (f32[512,1848]{0,1:T(8,128)S(1)}, f32[512,1848]{0,1:T(8,128)}, u32[]{:S(2)}) copy-start(f32[512,1848]{0,1:T(8,128)} %get-tuple-element.4) | copy-start | bytes 11354116
  253.9 3.6 %copy-start.9 = (bf16[512,1024]{1,0:T(8,128)(2,1)S(1)}, bf16[512,1024]{1,0:T(8,128)(2,1)}, u32[]{:S(2)}) copy-start(bf16[512,1024]{1,0:T(8,128)(2,1)} %all-gather.2.cloned.1.call-done) | copy-start | bytes 3145732
Sparse Core Ops, SparseCore 0:
  10.2 38.3 all-gather.1
  59.2 175.9 all-reduce.2
where the time goes:
time: 273 us; the launch traced here: 270 us
  waiting for transfers between devices  218 us (80%)
  matrix products  24.5 us (9%)
  between operations  14.1 us (5%)
  other arithmetic  7.55 us (3%)
  starting transfers between devices  4.09 us (1%)
    psum x1, waiting for transfers between devices, local(): gate, up, back = lax.psum((gate_part, up_part, back_part), 'dp')  176 us
    all_gather x1, waiting for transfers between devices, sent_together(): filled, at, outs = (lax.all_gather(both, axis, axis=dim, tiled=True), 0, [])  39.6 us
    dot_general x3, matrix products, contract_first(): lax.dot_general(left, right, (((0,), (0,)), ((), ())), preferred_element_...  10.4 us
    dot_general x3, matrix products, contract_last(): lax.dot_general(left, right, (((1,), (1,)), ((), ())), preferred_element_...  6.73 us
  transfers between devices with their start and end apart: 3, of which 3 were waited for; matrix products, arithmetic and copies ran while one was open for 4% of the time, Pallas kernels for 0%

commit v1 on v0

v1 whole, which is shorter than its diff:
```python
import jax
import jax.numpy as jnp
from jax import lax
from jax.sharding import PartitionSpec as P


def contract_last(left, right):
    return lax.dot_general(
        left, right, (((1,), (1,)), ((), ())), preferred_element_type=jnp.float32
    )


def contract_first(left, right):
    return lax.dot_general(
        left, right, (((0,), (0,)), ((), ())), preferred_element_type=jnp.float32
    )


def elementwise(gate, up, back):
    sig = jax.nn.sigmoid(gate)
    hidden = (gate * sig * up).astype(jnp.bfloat16)
    up_delta = (back * gate * sig).astype(jnp.bfloat16)
    gate_delta = (back * up * sig * (1.0 + gate * (1.0 - sig))).astype(jnp.bfloat16)
    return (hidden, gate_delta, up_delta)


def local(inputs, upstream, gate_weight, up_weight, down_weight):
    both = lax.all_gather(jnp.concatenate([inputs, upstream], 1), "blk", axis=0, tiled=True)
    width = inputs.shape[1]
    rows_all, grads_all = both[:, :width], both[:, width:]
    parts = [
        jnp.dot(rows_all, gate_weight, preferred_element_type=jnp.float32),
        jnp.dot(rows_all, up_weight, preferred_element_type=jnp.float32),
        contract_last(grads_all, down_weight),
    ]
    sums = [lax.psum_scatter(p, "dp", scatter_dimension=0, tiled=True) for p in parts]
    deltas = elementwise(*sums)
    hidden, gate_delta, up_delta = [
        lax.all_gather(d, "dp", axis=0, tiled=True) for d in deltas
    ]
    partial_input = contract_last(gate_delta, gate_weight) + contract_last(up_delta, up_weight)
    parts = partial_input.reshape(8, -1, width)
    input_grad = jnp.sum(lax.all_to_all(parts, "blk", 0, 0, tiled=True), axis=0)
    down_grad = contract_first(hidden, grads_all).astype(jnp.bfloat16)
    gate_grad = contract_first(rows_all, gate_delta).astype(jnp.bfloat16)
    up_grad = contract_first(rows_all, up_delta).astype(jnp.bfloat16)
    return (input_grad.astype(jnp.bfloat16), gate_grad, up_grad, down_grad)


def solution(mesh):
    return jax.shard_map(
        local,
        mesh=mesh,
        in_specs=(P("blk", "dp"), P("blk", "dp"), P("dp", "blk"), P("dp", "blk"), P("blk", "dp")),
        out_specs=(P("blk", "dp"), P("dp", "blk"), P("dp", "blk"), P("blk", "dp")),
        check_vma=False,
    )
```

time: 273 us -> 462 us (1.69)
  waiting for transfers between devices: 218 us -> 405 us
  matrix products: 24.5 us -> 31.7 us
    reduce_scatter x0 -> x3, waiting for transfers between devices: none -> 237 us  [local(): lax.psum_scatter(p, 'dp', scatter_dimension=0, tiled=True)]
    psum x1 -> x0, waiting for transfers between devices: 176 us -> none  [local(): gate, up, back = lax.psum((gate_part, up_part, back_part), 'dp')]
    all_gather x1 -> x4, waiting for transfers between devices: 39.6 us -> 167 us  [the longest x3 127 us: local(): lax.all_gather(d, 'dp', axis=0, tiled=True)]
    dot_general x3, matrix products: 6.73 us -> 13.2 us  [contract_last(): lax.dot_general(left, right, (((1,), (1,)), ((), ())), preferred_element_...]
  transfers between devices with their start and end apart: 3 -> 8, of which waited for: 3 -> 7; matrix products, arithmetic and copies ran while one was open for 4% -> 6% of each run, Pallas kernels for 0% -> 0%
where the time goes in v1:
time: 462 us
  waiting for transfers between devices  405 us (88%)
  matrix products  31.7 us (7%)
  between operations  14.2 us (3%)
  other arithmetic  5.63 us (1%)
    reduce_scatter x3, waiting for transfers between devices, local(): lax.psum_scatter(p, 'dp', scatter_dimension=0, tiled=True)  237 us
    all_gather x3, waiting for transfers between devices, local(): lax.all_gather(d, 'dp', axis=0, tiled=True)  127 us
    all_gather x1, waiting for transfers between devices, local(): lax.all_gather(jnp.concatenate([inputs, upstream], 1), 'blk', axis=0, til...  39.6 us
    dot_general x3, matrix products, contract_last(): lax.dot_general(left, right, (((1,), (1,)), ((), ())), preferred_element_...  13.2 us
    dot_general x3, matrix products, contract_first(): lax.dot_general(left, right, (((0,), (0,)), ((), ())), preferred_element_...  10.6 us
  transfers between devices with their start and end apart: 8, of which 7 were waited for; matrix products, arithmetic and copies ran while one was open for 6% of the time, Pallas kernels for 0%

profile of v1, /device:TPU:1, one launch (start us, length us, event | category | flops | bytes accessed | tf_op | source)
XLA Modules:
  0.0 462.0 jit_solution(15373133980176718704)
XLA Ops:
  7.2 1.7 pad_maximum_fusion
  8.9 0.0 reduce-scatter.4.cloned.1.call-start
  9.0 39.6 %all-gather.5.cloned.1.call-done = bf16[512,1024]{1,0:T(8,128)(2,1)} async-done(((bf16[64,1024]{1,0:T(8,128)(2,1)}), bf16[512,1024]{1,0:T(8,128)(2,1)}) %all-gather.5.cloned.1.call-update) | async-done | bytes 1048592 | tf_op jit(solution)/shard_map/all_gather | solution.py:28
  48.6 4.8 %fusion.1 = f32[512,1848]{1,0:T(8,128)} fusion(bf16[1848,512]{1,0:T(8,128)(2,1)} %param.9, bf16[512,1024]{1,0:T(8,128)(2,1)} %all-gather.5.cloned.1.call-done), kind=kOutput, calls=%fused_computation.5 | convolution fusion | flops 968884224 | bytes 6201344 | tf_op jit(solution)/shard_map/dot_general | solution.py:8
  53.5 1.1 copy-done.1
  54.7 4.7 %fusion.7 = f32[512,1848]{1,0:T(8,128)} fusion(bf16[512,1848]{0,1:T(8,128)(2,1)} %param.8, bf16[512,1024]{1,0:T(8,128)(2,1)S(1)} %copy-done.1), kind=kOutput, calls=%fused_computation.11 | convolution fusion | flops 968884224 | bytes 6201344 | tf_op jit(solution)/shard_map/dot_general | solution.py:33
  59.4 3.3 fusion.5
  62.7 0.0 all-gather.7.cloned.1.call-start
  62.7 72.9 %reduce-scatter.4.cloned.1.call-done = f32[32,1848]{1,0:T(8,128)} async-done(((f32[512,1848]{1,0:T(8,128)}), f32[32,1848]{1,0:T(8,128)}) %reduce-scatter.4.cloned.1.call-update) | async-done | bytes 236560 | tf_op jit(solution)/shard_map/reduce_scatter | solution.py:36
  135.7 81.9 %reduce-scatter.6.cloned.1.call-done = f32[32,1848]{1,0:T(8,128)} async-done(((f32[512,1848]{1,0:T(8,128)}), f32[32,1848]{1,0:T(8,128)}) %reduce-scatter.6.cloned.1.call-update) | async-done | bytes 236560 | tf_op jit(solution)/shard_map/reduce_scatter | solution.py:36
  217.6 81.8 %reduce-scatter.8.cloned.1.call-done = f32[32,1848]{1,0:T(8,128)} async-done(((f32[512,1848]{1,0:T(8,128)}), f32[32,1848]{1,0:T(8,128)}) %reduce-scatter.8.cloned.1.call-update) | async-done | bytes 236560 | tf_op jit(solution)/shard_map/reduce_scatter | solution.py:36
  299.4 2.0 multiply_convert_fusion
  301.5 0.5 all-gather.9.cloned.1.call-update
  302.1 0.7 all-gather.11.cloned.1.call-update
  302.8 47.4 %all-gather.7.cloned.1.call-done = bf16[512,1848]{1,0:T(8,128)(2,1)} async-done(((bf16[32,1848]{1,0:T(8,128)(2,1)}), bf16[512,1848]{1,0:T(8,128)(2,1)}) %all-gather.7.cloned.1.call-update) | async-done | bytes 1892368 | tf_op jit(solution)/shard_map/all_gather | solution.py:39
  350.2 3.8 fusion.9
  354.0 45.2 %all-gather.9.cloned.1.call-done = bf16[512,1848]{1,0:T(8,128)(2,1)} async-done(((bf16[32,1848]{1,0:T(8,128)(2,1)}), bf16[512,1848]{1,0:T(8,128)(2,1)}) %all-gather.9.cloned.1.call-update) | async-done | bytes 1892368 | tf_op jit(solution)/shard_map/all_gather | solution.py:39
  399.2 4.6 convolution_add_fusion
  403.8 4.2 all-to-all-start
  408.0 4.2 convolution_convert_fusion.1
  412.2 2.4 convolution_convert_fusion.2
  414.6 34.6 %all-gather.11.cloned.1.call-done = bf16[512,1848]{1,0:T(8,128)(2,1)} async-done(((bf16[32,1848]{1,0:T(8,128)(2,1)}), bf16[512,1848]{1,0:T(8,128)(2,1)}) %all-gather.11.cloned.1.call-update) | async-done | bytes 1892368 | tf_op jit(solution)/shard_map/all_gather | solution.py:39
  449.2 4.0 convolution_convert_fusion
  453.2 1.9 reduce_sum.9
  (16 shorter events, 0.3 us)
Async XLA Ops:
  7.2 52.2 %copy-start = (bf16[512,1848]{0,1:T(8,128)(2,1)S(1)}, bf16[512,1848]{0,1:T(8,128)(2,1)}, u32[]{:S(2)}) copy-start(bf16[512,1848]{0,1:T(8,128)(2,1)} %param.7) | copy-start | bytes 5677060
  7.2 41.4 %all-gather.5.cloned.1.call-start = ((), (), s32[]{:S(2)}) async-start(), calls=%async_computation.4 | async-start | bytes 1179648 | tf_op jit(solution)/shard_map/all_gather | solution.py:28
  8.9 126.8 %reduce-scatter.4.cloned.1.call-start = ((), (), s32[]{:S(2)}) async-start(), calls=%async_computation.5 | async-start | bytes 4177920 | tf_op jit(solution)/shard_map/reduce_scatter | solution.py:36
  53.4 1.2 copy-start.1
  53.5 164.2 %reduce-scatter.6.cloned.1.call-start = ((), (), s32[]{:S(2)}) async-start(), calls=%async_computation.6 | async-start | bytes 4177920 | tf_op jit(solution)/shard_map/reduce_scatter | solution.py:36
  59.4 240.1 %reduce-scatter.8.cloned.1.call-start = ((), (), s32[]{:S(2)}) async-start(), calls=%async_computation.7 | async-start | bytes 4177920 | tf_op jit(solution)/shard_map/reduce_scatter | solution.py:36
  62.7 287.5 %all-gather.7.cloned.1.call-start = ((), (), s32[]{:S(2)}) async-start(), calls=%async_computation.8 | async-start | bytes 2088960 | tf_op jit(solution)/shard_map/all_gather | solution.py:39
  301.5 97.7 %all-gather.9.cloned.1.call-start = ((), (), s32[]{:S(2)}) async-start(), calls=%async_computation.9 | async-start | bytes 2088960 | tf_op jit(solution)/shard_map/all_gather | solution.py:39
  302.1 147.1 %all-gather.11.cloned.1.call-start = ((), (), s32[]{:S(2)}) async-start(), calls=%async_computation.10 | async-start | bytes 2088960 | tf_op jit(solution)/shard_map/all_gather | solution.py:39
  403.8 49.4 %all-to-all-start = ((f32[8,64,512]{2,1,0:T(8,128)}), f32[8,64,512]{2,1,0:T(8,128)}, u32[]{:S(2)}, u32[]{:S(2)}) async-start(f32[8,64,512]{2,1,0:T(8,128)} %bitcast.11), calls=%async_computation.3 | async-start | bytes 2097152 | tf_op jit(solution)/shard_map/all_to_all | solution.py:43
  408.0 4.2 copy-start.2
Sparse Core Ops, SparseCore 0:
  10.2 38.3 all-gather.4
  53.6 82.0 reduce-scatter.3
  139.8 77.7 reduce-scatter.5
  221.6 77.7 reduce-scatter.7
  302.3 47.8 all-gather.6
  353.1 46.0 all-gather.8
  401.7 47.4 all-gather.10

commit v2 on v1

v2 whole, which is shorter than its diff:
```python
import jax
import jax.numpy as jnp
from jax import lax
from jax.experimental import pallas as pl
from jax.experimental.pallas import tpu as pltpu
from jax.sharding import PartitionSpec as P

BF = jnp.bfloat16
F32 = jnp.float32
TAIL = 896
HALF = 1024
OFFSETS = (0, 3, 1, 2)


def contract_last(left, right):
    return lax.dot_general(
        left, right, (((1,), (1,)), ((), ())), preferred_element_type=F32
    )


def contract_first(left, right):
    return lax.dot_general(
        left, right, (((0,), (0,)), ((), ())), preferred_element_type=F32
    )


def kernel(
    inputs, upstream, gate_w, up_w, down_w,
    ig_out, deltas_out, rows_out,
    xin, wf, wl, part, rs_in, rs_out, x_in, x_out, tail, deltas, ig_in, ig_send, ig_val,
    loc_sem, w_send, w_recv,
    in_send, in_recv, pair_send, pair_recv,
    rs_ssem, rs_recv, x_send, x_recv,
    g_send, g_recv, gp_send, gp_recv, ig_ssem, ig_rsem,
):
    ff = gate_w.shape[1]
    rest = ff - HALF
    d = inputs.shape[1]
    dp = lax.axis_index("dp")
    blk = lax.axis_index("blk")
    core = lax.rem(dp, 2)
    z = lax.rem(lax.div(dp, 2), 4)
    xh = lax.div(dp, 8)
    y = lax.div(blk, 2)
    xl = lax.rem(blk, 2)

    def at(dp_=None, blk_=None):
        return {"dp": dp if dp_ is None else dp_, "blk": blk if blk_ is None else blk_}

    def dpi(xh_, z_, core_):
        return (xh_ * 4 + z_) * 2 + core_

    def m4(v):
        return lax.rem(v + 4, 4)

    pair = at(dp_=dpi(xh, z, 1 - core))
    zp = at(dp_=dpi(xh, m4(z + 1), core))
    zm = at(dp_=dpi(xh, m4(z - 1), core))
    xo = at(dp_=dpi(1 - xh, z, core))
    xlo = at(blk_=y * 2 + 1 - xl)
    yp = at(blk_=m4(y + 1) * 2 + xl)
    ym = at(blk_=m4(y - 1) * 2 + xl)
    others = [at(blk_=m4(y + o) * 2 + q) for o in (1, 2, 3) for q in (0, 1)]

    def mo(v, n):
        return pl.multiple_of(v, n)

    def send(src, dst, ssem, rsem, dev):
        c = pltpu.make_async_remote_copy(
            src_ref=src, dst_ref=dst, send_sem=ssem, recv_sem=rsem,
            device_id=dev, device_id_type=pl.DeviceIdType.MESH,
        )
        c.start()
        return c

    wf[0, :, TAIL:] = jnp.zeros((2 * d, HALF - TAIL), BF)
    wf[1, :, TAIL:] = jnp.zeros((2 * d, HALF - TAIL), BF)
    wf[2, HALF - 256:, :] = jnp.zeros((256, 2 * d), BF)

    own_in = [
        pltpu.make_async_copy(
            src, xin.at[a, pl.ds(mo(blk * 64, 64), 64), pl.ds(mo(core * d, 512), d)], loc_sem.at[a]
        )
        for a, src in enumerate((inputs, upstream))
    ]
    for c in own_in:
        c.start()

    barrier = pltpu.get_barrier_semaphore()
    peers = [pair, zp, zm, xo, xlo] + others
    for p in peers:
        pl.semaphore_signal(barrier, inc=1, device_id=p, device_id_type=pl.DeviceIdType.MESH)
    pl.semaphore_wait(barrier, len(peers))

    def piece(rows_blk, core_, a=None):
        r = pl.ds(mo(rows_blk * 64, 64), 64)
        c = pl.ds(mo(core_ * d, 512), d)
        return xin.at[:, r, c] if a is None else xin.at[pl.ds(a, 1), r, c]

    sends = []

    def arrived(ref, sem):
        pltpu.make_async_copy(ref, ref, sem).wait()

    for c in own_in:
        c.wait()
    mine = piece(blk, core)
    sends.append(send(mine, mine, in_send.at[0], in_recv.at[0], xlo))
    sends.append(send(mine, mine, in_send.at[1], in_recv.at[1], yp))
    sends.append(send(mine, mine, in_send.at[2], in_recv.at[2], ym))
    sends.append(send(mine, mine, pair_send.at[0], pair_recv.at[0], pair))

    full = [
        pltpu.make_async_copy(src, wl.at[a], loc_sem.at[5 + a])
        for a, src in enumerate((gate_w, up_w))
    ]
    for c in full:
        c.start()
    my_rows = pl.ds(mo(core * d, 512), d)

    def down_copies(keep, give):
        local_ = pltpu.make_async_copy(
            down_w.at[pl.ds(*keep), :], wf.at[2, pl.ds(0, keep[1]), my_rows], loc_sem.at[4]
        )
        away = pltpu.make_async_remote_copy(
            src_ref=down_w.at[pl.ds(*give), :], dst_ref=wf.at[2, pl.ds(0, give[1]), my_rows],
            send_sem=w_send.at[2], recv_sem=w_recv.at[2],
            device_id=pair, device_id_type=pl.DeviceIdType.MESH,
        )
        return local_, away

    def head(a, hbm):
        return hbm.at[:, pl.ds(0, HALF)], wf.at[a, my_rows, :]

    heads = (gate_w, up_w)

    @pl.when(core == 0)
    def _():
        for c in down_copies((0, HALF), (HALF, rest)):
            c.start()
        for a in (0, 1):
            pltpu.make_async_copy(*head(a, heads[a]), loc_sem.at[2 + a]).start()
        for a in (0, 1):
            full[a].wait()
            tail[a, :, TAIL - 128:] = jnp.zeros((d, 128), BF)
            tail[a, :, :rest] = wl[a, :, HALF:]
            send(tail.at[a], wf.at[a, my_rows, pl.ds(0, TAIL)], w_send.at[a], w_recv.at[a], pair)

    @pl.when(core == 1)
    def _():
        for c in down_copies((HALF, rest), (0, HALF)):
            c.start()
        for a in (0, 1):
            src, dst = head(a, heads[a])
            send(src, dst, w_send.at[a], w_recv.at[a], pair)
        for a in (0, 1):
            full[a].wait()
            wf[a, my_rows, TAIL - 128:TAIL] = jnp.zeros((d, 128), BF)
            wf[a, my_rows, :rest] = wl[a, :, HALF:]

    pb = y * 2 + 1 - xl
    other = piece(pb, core)
    arrived(other, in_recv.at[0])
    sends.append(send(other, other, in_send.at[3], in_recv.at[3], yp))
    sends.append(send(other, other, in_send.at[4], in_recv.at[4], ym))
    sends.append(send(other, other, pair_send.at[1], pair_recv.at[1], pair))

    def from_neighbours(q, s_yp, s_ym, base):
        bm = m4(y - 1) * 2 + q
        bp = m4(y + 1) * 2 + q
        arrived(piece(bm, core), in_recv.at[s_yp])
        f = piece(bm, core, 0)
        sends.append(send(f, f, in_send.at[base], in_recv.at[base], yp))
        arrived(piece(bp, core), in_recv.at[s_ym])
        f = piece(bp, core, 1)
        sends.append(send(f, f, in_send.at[base + 1], in_recv.at[base + 1], ym))
        i = base - 5
        sends.append(send(piece(bm, core), piece(bm, core), pair_send.at[2 + i], pair_recv.at[2 + i], pair))
        sends.append(send(piece(bp, core), piece(bp, core), pair_send.at[3 + i], pair_recv.at[3 + i], pair))

    def from_far(q, base, i):
        b2 = m4(y + 2) * 2 + q
        for a in (0, 1):
            arrived(piece(b2, core, a), in_recv.at[base + a])
        sends.append(send(piece(b2, core), piece(b2, core), pair_send.at[i], pair_recv.at[i], pair))

    def wait_pair(k):
        qs = (xl, 1 - xl)
        idx = ((0, 1), (2, 4), (3, 5), (6, 7))[k]
        for q, i in zip(qs, idx):
            ref = piece(m4(y + OFFSETS[k]) * 2 + q, 1 - core)
            arrived(ref, pair_recv.at[i])

    def rows_of(k):
        return mo(m4(y + OFFSETS[k]) * 128, 128)

    def forward(k):
        wait_pair(k)
        r = pl.ds(rows_of(k), 128)
        part[k, 0] = jnp.dot(xin[0, r, :], wf[0], preferred_element_type=F32)
        part[k, 1] = jnp.dot(xin[0, r, :], wf[1], preferred_element_type=F32)
        part[k, 2] = contract_last(xin[1, r, :], wf[2])

    def own(k, zd, half):
        return part[k, :, pl.ds(mo(zd * 32 + half * 16, 16), 16), :]

    def rs_send(k, dr, n, val, dev):
        rs_out[k, dr, n] = val.astype(BF)
        sends.append(send(
            rs_out.at[k, dr, n], rs_in.at[k, dr, n], rs_ssem.at[k, dr, n], rs_recv.at[k, dr, n], dev
        ))

    def reduce_first(k):
        for n, far in ((0, 1), (1, 0)):
            for dr, (sign, dev) in enumerate(((1, zp), (-1, zm))):
                zd = m4(z + 2) if far else m4(z + sign)
                rs_send(k, dr, n, own(k, zd, dr if far else 1 - dr), dev)

    def reduce_next(k):
        for dr, (sign, dev) in enumerate(((1, zp), (-1, zm))):
            arrived(rs_in.at[k, dr, 0], rs_recv.at[k, dr, 0])
            rs_send(k, dr, 2, own(k, m4(z + sign), dr) + rs_in[k, dr, 0].astype(F32), dev)

    def chip_sum(k, q):
        return own(k, z, q) + rs_in[k, q, 2].astype(F32) + rs_in[k, 1 - q, 1].astype(F32)

    def reduce_last(k):
        for n in (1, 2):
            for dr in (0, 1):
                arrived(rs_in.at[k, dr, n], rs_recv.at[k, dr, n])
        x_out[k] = chip_sum(k, 1 - xh).astype(BF)
        sends.append(send(x_out.at[k], x_in.at[k], x_send.at[k], x_recv.at[k], xo))

    def tile(k, z_, xh_, rows=16, core_=None):
        c = core if core_ is None else core_
        return deltas.at[
            :,
            pl.ds(mo(rows_of(k) + z_ * 32 + xh_ * 16, 16), rows),
            pl.ds(mo(c * HALF, HALF), HALF),
        ]

    def g_out(k, n, t, rsem, dev):
        sends.append(send(t, t, g_send.at[k, n], g_recv.at[k, rsem], dev))

    def g_pair(k, n, z_):
        t = tile(k, z_, 0, 32)
        sends.append(send(t, t, gp_send.at[k, n], gp_recv.at[k, n], pair))

    def elementwise(k):
        arrived(x_in.at[k], x_recv.at[k])
        sums = chip_sum(k, xh) + x_in[k].astype(F32)
        gate, up, back = sums[0], sums[1], sums[2]
        sig = 1.0 / (1.0 + jnp.exp(-gate))
        gs = gate * sig
        hidden = gs * up
        up_delta = back * gs
        gate_delta = back * up * sig * (1.0 + gate * (1.0 - sig))
        r = pl.ds(mo(rows_of(k) + z * 32 + xh * 16, 16), 16)
        c = pl.ds(mo(core * HALF, HALF), HALF)
        deltas[0, r, c] = hidden.astype(BF)
        deltas[1, r, c] = gate_delta.astype(BF)
        deltas[2, r, c] = up_delta.astype(BF)
        t = tile(k, z, xh)
        g_out(k, 0, t, 0, xo)
        g_out(k, 1, t, 1 + xh, zp)
        g_out(k, 2, t, 3 + xh, zm)

    def gather_x(k):
        t = tile(k, z, 1 - xh)
        arrived(t, g_recv.at[k, 0])
        g_out(k, 3, t, 1 + 1 - xh, zp)
        g_out(k, 4, t, 3 + 1 - xh, zm)
        g_pair(k, 0, z)

    def neighbour_tile(k, xq, n):
        for i, zz in enumerate((m4(z - 1), m4(z + 1))):
            arrived(tile(k, zz, xq), g_recv.at[k, 1 + 2 * i + xq])
        src = tile(k, m4(z - 1 + 2 * xq), xq)
        dev = at(dp_=dpi(xh, m4(z + 1 - 2 * xq), core))
        g_out(k, n, src, 5 + xq, dev)

    def gather_near(k):
        neighbour_tile(k, xh, 5)

    def gather_next(k):
        neighbour_tile(k, 1 - xh, 6)
        g_pair(k, 1, m4(z - 1))
        g_pair(k, 2, m4(z + 1))

    def gather_far(k):
        for q in (0, 1):
            arrived(tile(k, m4(z + 2), q), g_recv.at[k, 5 + q])
        g_pair(k, 3, m4(z + 2))

    outs = []

    def backward(k):
        for n, zz in enumerate((z, m4(z - 1), m4(z + 1), m4(z + 2))):
            arrived(tile(k, zz, 0, 32, 1 - core), gp_recv.at[k, n])
        r = pl.ds(rows_of(k), 128)
        c = pltpu.make_async_copy(deltas.at[:, r, :], deltas_out.at[:, r, :], loc_sem.at[7 + k])
        c.start()
        outs.append(c)
        ig = contract_last(deltas[1, r, :ff], wl[0]) + contract_last(deltas[2, r, :ff], wl[1])
        if k == 0:
            ig_val[...] = ig
            ig_send[k] = ig.astype(BF)
            q = 1 - xl
            sends.append(send(
                ig_send.at[k, pl.ds(mo(q * 64, 64), 64)], ig_in.at[xl],
                ig_ssem.at[k, 0], ig_rsem.at[xl], at(blk_=y * 2 + q),
            ))
        else:
            ig_send[k] = ig.astype(BF)
            for q in (0, 1):
                sends.append(send(
                    ig_send.at[k, pl.ds(q * 64, 64)], ig_in.at[2 * k + xl],
                    ig_ssem.at[k, q], ig_rsem.at[2 * k + xl], at(blk_=m4(y + OFFSETS[k]) * 2 + q),
                ))

    def ready_weights():
        their_rows = pl.ds(mo((1 - core) * d, 512), d)

        def settle(keep, give):
            local_, away = down_copies(keep, give)
            local_.wait()
            away.wait_send()
            arrived(wf.at[2, pl.ds(0, keep[1]), their_rows], w_recv.at[2])

        @pl.when(core == 0)
        def _():
            settle((0, HALF), (HALF, rest))
            for a in (0, 1):
                pltpu.make_async_copy(*head(a, heads[a]), loc_sem.at[2 + a]).wait()
                arrived(wf.at[a, their_rows, :], w_recv.at[a])
                arrived(tail.at[a], w_send.at[a])

        @pl.when(core == 1)
        def _():
            settle((HALF, rest), (0, HALF))
            for a in (0, 1):
                arrived(wf.at[a, their_rows, pl.ds(0, TAIL)], w_recv.at[a])
                arrived(wf.at[a, my_rows, :], w_send.at[a])

    from_neighbours(xl, 1, 2, 5)
    ready_weights()
    forward(0)
    reduce_first(0)
    from_neighbours(1 - xl, 3, 4, 7)
    forward(1)
    reduce_first(1)
    reduce_next(0)
    forward(2)
    reduce_first(2)
    from_far(xl, 5, 6)
    from_far(1 - xl, 7, 7)
    reduce_next(1)
    forward(3)
    reduce_first(3)
    reduce_last(0)
    c = pltpu.make_async_copy(xin.at[:, :, pl.ds(mo(core * d, 512), d)], rows_out, loc_sem.at[11])
    c.start()
    outs.append(c)
    chain = [
        reduce_next, reduce_last, elementwise, gather_x, gather_near, gather_next, gather_far, backward,
    ]
    done = [2, 1, 0, 0]
    for tick in range(len(chain) + 3):
        for k in range(4):
            i = tick - k
            if 0 <= i < len(chain) and i >= done[k]:
                chain[i](k)

    for k in range(4):
        for q in (0, 1):
            i = 2 * k + (q if k else 0)
            if k == 0:
                if q == 0:
                    arrived(ig_in.at[1 - xl], ig_rsem.at[1 - xl])
            else:
                arrived(ig_in.at[i], ig_rsem.at[i])
    total = ig_val[pl.ds(mo(xl * 64, 64), 64), :] + ig_in[1 - xl].astype(F32)
    for i in range(2, 8):
        total = total + ig_in[i].astype(F32)
    ig_out[...] = total.astype(BF)
    for c in sends:
        c.wait_send()
    for c in outs:
        c.wait()


def fused(inputs, upstream, gate_w, up_w, down_w):
    d = inputs.shape[1]
    any_ = pl.BlockSpec(memory_space=pl.ANY)
    dma = pltpu.SemaphoreType.DMA
    return pl.pallas_call(
        kernel,
        name="fused",
        out_shape=(
            jax.ShapeDtypeStruct((64, d), BF),
            jax.ShapeDtypeStruct((3, 512, 2 * HALF), BF),
            jax.ShapeDtypeStruct((2, 512, d), BF),
        ),
        in_specs=[any_] * 5,
        out_specs=(pl.BlockSpec(memory_space=pltpu.VMEM), any_, any_),
        scratch_shapes=[
            pltpu.VMEM((2, 512, 2 * d), BF),
            pltpu.VMEM((3, HALF, HALF), BF),
            pltpu.VMEM((2, d, gate_w.shape[1]), BF),
            pltpu.VMEM((4, 3, 128, HALF), F32),
            pltpu.VMEM((4, 2, 3, 3, 16, HALF), BF),
            pltpu.VMEM((4, 2, 3, 3, 16, HALF), BF),
            pltpu.VMEM((4, 3, 16, HALF), BF),
            pltpu.VMEM((4, 3, 16, HALF), BF),
            pltpu.VMEM((2, d, TAIL), BF),
            pltpu.VMEM((3, 512, 2 * HALF), BF),
            pltpu.VMEM((8, 64, d), BF),
            pltpu.VMEM((4, 128, d), BF),
            pltpu.VMEM((128, d), F32),
            dma((12,)), dma((3,)), dma((3,)),
            dma((9,)), dma((9,)), dma((8,)), dma((8,)),
            dma((4, 2, 3)), dma((4, 2, 3)), dma((4,)), dma((4,)),
            dma((4, 7)), dma((4, 7)), dma((4, 4)), dma((4, 4)), dma((4, 2)), dma((8,)),
        ],
        compiler_params=pltpu.CompilerParams(
            collective_id=0, has_side_effects=True, vmem_limit_bytes=60 * 1024 * 1024
        ),
        cost_estimate=pl.CostEstimate(flops=5 * 10**9, bytes_accessed=20 * 10**6, transcendentals=10**6),
    )(inputs, upstream, gate_w, up_w, down_w)


def grads_kernel(rows, deltas, gate_ref, up_ref, down_ref):
    gate_ref[...] = contract_first(rows[0], deltas[1]).astype(BF)
    up_ref[...] = contract_first(rows[0], deltas[2]).astype(BF)
    down_ref[...] = contract_first(deltas[0], rows[1]).astype(BF)


def weight_grads(rows, deltas, ff):
    d = rows.shape[2]
    n = 512
    return pl.pallas_call(
        grads_kernel,
        name="weight_grads",
        grid=(pl.cdiv(ff, n),),
        out_shape=(
            jax.ShapeDtypeStruct((d, ff), BF),
            jax.ShapeDtypeStruct((d, ff), BF),
            jax.ShapeDtypeStruct((ff, d), BF),
        ),
        in_specs=[
            pl.BlockSpec((2, 512, d), lambda i: (0, 0, 0)),
            pl.BlockSpec((3, 512, n), lambda i: (0, 0, i)),
        ],
        out_specs=(
            pl.BlockSpec((d, n), lambda i: (0, i)),
            pl.BlockSpec((d, n), lambda i: (0, i)),
            pl.BlockSpec((n, d), lambda i: (i, 0)),
        ),
        compiler_params=pltpu.CompilerParams(vmem_limit_bytes=40 * 1024 * 1024),
    )(rows, deltas)


def local(inputs, upstream, gate_weight, up_weight, down_weight):
    input_grad, deltas, rows = fused(inputs, upstream, gate_weight, up_weight, down_weight)
    gate_grad, up_grad, down_grad = weight_grads(rows, deltas, gate_weight.shape[1])
    return (input_grad, gate_grad, up_grad, down_grad)


def solution(mesh):
    return jax.shard_map(
        local,
        mesh=mesh,
        in_specs=(P("blk", "dp"), P("blk", "dp"), P("dp", "blk"), P("dp", "blk"), P("blk", "dp")),
        out_specs=(P("blk", "dp"), P("dp", "blk"), P("dp", "blk"), P("blk", "dp")),
        check_vma=False,
    )
```

time: 462 us -> 105 us (0.23)
  waiting for transfers between devices: 405 us -> 0 us
  Pallas kernels: 0 us -> 85 us
  matrix products: 31.7 us -> 0 us
  local copies, waits for them, and re-layouts: 1.16 us -> 18.8 us
  between operations: 14.2 us -> 0.66 us
  other arithmetic: 5.63 us -> 0 us
    reduce_scatter x3 -> x0, waiting for transfers between devices: 237 us -> none  [local(): lax.psum_scatter(p, 'dp', scatter_dimension=0, tiled=True)]
    all_gather x4 -> x0, waiting for transfers between devices: 167 us -> none  [the longest x3 127 us: local(): lax.all_gather(d, 'dp', axis=0, tiled=True)]
    pallas_call x0 -> x2, Pallas kernels: none -> 85 us  [the longest x1 79.2 us: fused(): pl.pallas_call(kernel, name='fused', out_shape=(jax.ShapeDtypeStruct((64,...]
    dot_general x8 -> x0, matrix products: 31.7 us -> none  [the longest x3 13.2 us: contract_last(): lax.dot_general(left, right, (((1,), (1,)), ((), ())), preferred_element_...]
    unnamed x6 -> x15, local copies, waits for them, and re-layouts: 1.16 us -> 18.8 us
  transfers between devices with their start and end apart: 8 -> 0, of which waited for: 7 -> 0; matrix products, arithmetic and copies ran while one was open for 6% -> 0% of each run, Pallas kernels for 0% -> 0%
where the time goes in v2:
time: 105 us; the launch traced here: 104 us
  Pallas kernels  85 us (81%)
  local copies, waits for them, and re-layouts  18.8 us (18%)
    pallas_call x1, Pallas kernels, fused(): pl.pallas_call(kernel, name='fused', out_shape=(jax.ShapeDtypeStruct((64,...  79.2 us
    unnamed x15, local copies, waits for them, and re-layouts  18.8 us
    pallas_call x1, Pallas kernels, weight_grads(): pl.pallas_call(grads_kernel, name='weight_grads', grid=(pl.cdiv(ff, n),),...  5.8 us

profile of v2, /device:TPU:1, one launch (start us, length us, event | category | flops | bytes accessed | tf_op | source)
XLA Modules:
  0.0 104.5 jit_solution(4145638992168289315)
XLA Ops:
  0.6 0.0 copy-start.3
  0.6 4.1 %copy.9.gate_w = bf16[512,1848]{1,0:T(8,128)(2,1)} copy(bf16[512,1848]{0,1:T(8,128)(2,1)} %param.7) | data formatting | bytes 3784704 | tf_op args[2]
  4.7 0.0 copy-done.3
  4.7 2.6 %copy.10.up_w = bf16[512,1848]{1,0:T(8,128)(2,1)} copy(bf16[512,1848]{0,1:T(8,128)(2,1)S(1)} %copy-done.3) | data formatting | bytes 3784704 | tf_op args[3]
  7.3 79.2 %fused.1 = (bf16[64,512]{1,0:T(8,128)(2,1)}, bf16[3,512,2048]{2,1,0:T(8,128)(2,1)}, bf16[2,512,512]{2,1,0:T(8,128)(2,1)}) custom-call(bf16[64,512]{1,0:T(8,128)(2,1)} %inputs.1, bf16[64,512]{1,0:T(8,128)(2,1)} %upstream.1, bf16[512,1848]{1,0:T(8,128)(2,1)} %copy.9.gate_w, bf16[512,1848]{1,0:T(8,128)(2,1)} %copy.10.up_w, bf16[1848,512]{1,0:T(8,128)(2,1)} %down_w.1), custom_call_target="tpu_custom_call" | custom-call | flops 5000000000 | bytes 20000000 | tf_op jit(solution)/shard_map/fused/pallas_call | solution.py:396
  86.5 0.0 copy-start
  86.5 2.8 %copy-done = bf16[3,512,2048]{2,1,0:T(8,128)(2,1)S(1)} copy-done((bf16[3,512,2048]{2,1,0:T(8,128)(2,1)S(1)}, bf16[3,512,2048]{2,1,0:T(8,128)(2,1)}, u32[]{:S(2)}) %copy-start) | copy-done | bytes 6291480
  89.3 0.0 copy-start.2
  89.3 1.2 %copy-done.2 = bf16[2,512,512]{2,1,0:T(8,128)(2,1)S(1)} copy-done((bf16[2,512,512]{2,1,0:T(8,128)(2,1)S(1)}, bf16[2,512,512]{2,1,0:T(8,128)(2,1)}, u32[]{:S(2)}) %copy-start.2) | copy-done | bytes 1048600
  90.5 5.8 %weight_grads.1 = (bf16[512,1848]{1,0:T(8,128)(2,1)S(1)}, bf16[512,1848]{1,0:T(8,128)(2,1)S(1)}, bf16[1848,512]{1,0:T(8,128)(2,1)}) custom-call(bf16[2,512,512]{2,1,0:T(8,128)(2,1)S(1)} %copy-done.2, bf16[3,512,2048]{2,1,0:T(8,128)(2,1)S(1)} %copy-done), custom_call_target="tpu_custom_call" | custom-call | tf_op jit(solution)/shard_map/weight_grads/pallas_call | solution.py:441
  96.3 0.0 copy-start.1
  96.3 1.3 %copy-done.1 = bf16[512,1848]{1,0:T(8,128)(2,1)} copy-done((bf16[512,1848]{1,0:T(8,128)(2,1)}, bf16[512,1848]{1,0:T(8,128)(2,1)S(1)}, u32[]{:S(2)}) %copy-start.1) | copy-done | bytes 1892376
  97.6 4.0 %copy.11 = bf16[512,1848]{0,1:T(8,128)(2,1)} copy(bf16[512,1848]{1,0:T(8,128)(2,1)} %copy-done.1) | data formatting | bytes 3784704
  101.6 0.0 copy-start.4
  101.6 2.3 %copy.12 = bf16[512,1848]{0,1:T(8,128)(2,1)} copy(bf16[512,1848]{1,0:T(8,128)(2,1)S(1)} %get-tuple-element.18) | data formatting | bytes 3784704
  103.8 0.0 copy-done.4
  103.8 0.6 copy.14
Async XLA Ops:
  0.6 4.1 %copy-start.3 = (bf16[512,1848]{0,1:T(8,128)(2,1)S(1)}, bf16[512,1848]{0,1:T(8,128)(2,1)}, u32[]{:S(2)}) copy-start(bf16[512,1848]{0,1:T(8,128)(2,1)} %param.8) | copy-start | bytes 5677060
  86.5 2.8 %copy-start = (bf16[3,512,2048]{2,1,0:T(8,128)(2,1)S(1)}, bf16[3,512,2048]{2,1,0:T(8,128)(2,1)}, u32[]{:S(2)}) copy-start(bf16[3,512,2048]{2,1,0:T(8,128)(2,1)} %get-tuple-element.12.deltas) | copy-start | bytes 18874372
  89.3 1.2 %copy-start.2 = (bf16[2,512,512]{2,1,0:T(8,128)(2,1)S(1)}, bf16[2,512,512]{2,1,0:T(8,128)(2,1)}, u32[]{:S(2)}) copy-start(bf16[2,512,512]{2,1,0:T(8,128)(2,1)} %get-tuple-element.11.rows) | copy-start | bytes 3145732
  96.3 1.3 %copy-start.1 = (bf16[512,1848]{1,0:T(8,128)(2,1)}, bf16[512,1848]{1,0:T(8,128)(2,1)S(1)}, u32[]{:S(2)}) copy-start(bf16[512,1848]{1,0:T(8,128)(2,1)S(1)} %get-tuple-element.17) | copy-start | bytes 5677060
  101.6 2.3 %copy-start.4 = (bf16[64,512]{1,0:T(8,128)(2,1)S(1)}, bf16[64,512]{1,0:T(8,128)(2,1)}, u32[]{:S(2)}) copy-start(bf16[64,512]{1,0:T(8,128)(2,1)} %get-tuple-element.24) | copy-start | bytes 196612

commit v3 on v2

--- a/solution.py
+++ b/solution.py
@@ -1,3 +1,5 @@
+import functools
+
 import jax
 import jax.numpy as jnp
 from jax import lax
@@ -7,8 +9,8 @@
 
 BF = jnp.bfloat16
 F32 = jnp.float32
-TAIL = 896
 HALF = 1024
+REST = 896
 OFFSETS = (0, 3, 1, 2)
 
 
@@ -24,16 +26,20 @@
     )
 
 
+def dot(left, right):
+    return jnp.dot(left, right, preferred_element_type=F32)
+
+
 def kernel(
     inputs, upstream, gate_w, up_w, down_w,
     ig_out, deltas_out, rows_out,
-    xin, wf, wl, part, rs_in, rs_out, x_in, x_out, tail, deltas, ig_in, ig_send, ig_val,
+    xin, wf, wl, part, rs_in, rs_out, x_in, x_out, deltas, ig_in, ig_send, ig_val,
     loc_sem, w_send, w_recv,
     in_send, in_recv, pair_send, pair_recv,
     rs_ssem, rs_recv, x_send, x_recv,
     g_send, g_recv, gp_send, gp_recv, ig_ssem, ig_rsem,
 ):
-    ff = gate_w.shape[1]
+    ff = gate_w.shape[0]
     rest = ff - HALF
     d = inputs.shape[1]
     dp = lax.axis_index("dp")
@@ -73,9 +79,8 @@
         c.start()
         return c
 
-    wf[0, :, TAIL:] = jnp.zeros((2 * d, HALF - TAIL), BF)
-    wf[1, :, TAIL:] = jnp.zeros((2 * d, HALF - TAIL), BF)
-    wf[2, HALF - 256:, :] = jnp.zeros((256, 2 * d), BF)
+    for a in range(3):
+        wf[a, HALF - 256:, :] = jnp.zeros((256, 2 * d), BF)
 
     own_in = [
         pltpu.make_async_copy(
@@ -98,6 +103,7 @@
         return xin.at[:, r, c] if a is None else xin.at[pl.ds(a, 1), r, c]
 
     sends = []
+    part_sends = []
 
     def arrived(ref, sem):
         pltpu.make_async_copy(ref, ref, sem).wait()
@@ -110,53 +116,36 @@
     sends.append(send(mine, mine, in_send.at[2], in_recv.at[2], ym))
     sends.append(send(mine, mine, pair_send.at[0], pair_recv.at[0], pair))
 
+    hbm = (gate_w, up_w, down_w)
     full = [
-        pltpu.make_async_copy(src, wl.at[a], loc_sem.at[5 + a])
-        for a, src in enumerate((gate_w, up_w))
+        pltpu.make_async_copy(hbm[a], wl.at[a], loc_sem.at[5 + a]) for a in (0, 1)
     ]
-    for c in full:
-        c.start()
     my_rows = pl.ds(mo(core * d, 512), d)
-
-    def down_copies(keep, give):
+    their_rows = pl.ds(mo((1 - core) * d, 512), d)
+
+    def weight_copies(a, keep, give):
         local_ = pltpu.make_async_copy(
-            down_w.at[pl.ds(*keep), :], wf.at[2, pl.ds(0, keep[1]), my_rows], loc_sem.at[4]
+            hbm[a].at[pl.ds(*keep), :], wf.at[a, pl.ds(0, keep[1]), my_rows], loc_sem.at[2 + a]
         )
         away = pltpu.make_async_remote_copy(
-            src_ref=down_w.at[pl.ds(*give), :], dst_ref=wf.at[2, pl.ds(0, give[1]), my_rows],
-            send_sem=w_send.at[2], recv_sem=w_recv.at[2],
+            src_ref=hbm[a].at[pl.ds(*give), :], dst_ref=wf.at[a, pl.ds(0, give[1]), my_rows],
+            send_sem=w_send.at[a], recv_sem=w_recv.at[a],
             device_id=pair, device_id_type=pl.DeviceIdType.MESH,
         )
         return local_, away
 
-    def head(a, hbm):
-        return hbm.at[:, pl.ds(0, HALF)], wf.at[a, my_rows, :]
-
-    heads = (gate_w, up_w)
-
-    @pl.when(core == 0)
-    def _():
-        for c in down_copies((0, HALF), (HALF, rest)):
-            c.start()
-        for a in (0, 1):
-            pltpu.make_async_copy(*head(a, heads[a]), loc_sem.at[2 + a]).start()
-        for a in (0, 1):
-            full[a].wait()
-            tail[a, :, TAIL - 128:] = jnp.zeros((d, 128), BF)
-            tail[a, :, :rest] = wl[a, :, HALF:]
-            send(tail.at[a], wf.at[a, my_rows, pl.ds(0, TAIL)], w_send.at[a], w_recv.at[a], pair)
-
-    @pl.when(core == 1)
-    def _():
-        for c in down_copies((HALF, rest), (0, HALF)):
-            c.start()
-        for a in (0, 1):
-            src, dst = head(a, heads[a])
-            send(src, dst, w_send.at[a], w_recv.at[a], pair)
-        for a in (0, 1):
-            full[a].wait()
-            wf[a, my_rows, TAIL - 128:TAIL] = jnp.zeros((d, 128), BF)
-            wf[a, my_rows, :rest] = wl[a, :, HALF:]
+    def on_core(body):
+        for c_, args in enumerate((((0, HALF), (HALF, rest)), ((HALF, rest), (0, HALF)))):
+            pl.when(core == c_)(functools.partial(body, *args))
+
+    def start_weights(keep, give):
+        for a in range(3):
+            for c in weight_copies(a, keep, give):
+                c.start()
+
+    on_core(start_weights)
+    for c in full:
+        c.start()
 
     pb = y * 2 + 1 - xl
     other = piece(pb, core)
@@ -197,18 +186,39 @@
     def forward(k):
         wait_pair(k)
         r = pl.ds(rows_of(k), 128)
-        part[k, 0] = jnp.dot(xin[0, r, :], wf[0], preferred_element_type=F32)
-        part[k, 1] = jnp.dot(xin[0, r, :], wf[1], preferred_element_type=F32)
+        part[k, 0] = contract_last(xin[0, r, :], wf[0])
+        part[k, 1] = contract_last(xin[0, r, :], wf[1])
         part[k, 2] = contract_last(xin[1, r, :], wf[2])
 
     def own(k, zd, half):
         return part[k, :, pl.ds(mo(zd * 32 + half * 16, 16), 16), :]
 
+    def each_width(body):
+        for c_, width in enumerate((HALF, REST)):
+            pl.when(core == c_)(functools.partial(body, c_, width))
+
+    def send_part(src, dst, ssem, rsem, dev):
+        def copy(c_, width):
+            return pltpu.make_async_remote_copy(
+                src_ref=src(c_, width), dst_ref=dst(c_, width), send_sem=ssem, recv_sem=rsem,
+                device_id=dev, device_id_type=pl.DeviceIdType.MESH,
+            )
+
+        each_width(lambda c_, width: copy(c_, width).start())
+        part_sends.append(copy)
+
+    def part_arrived(ref, sem):
+        each_width(lambda c_, width: arrived(ref(c_, width), sem))
+
+    def lanes(ref):
+        return lambda c_, width: ref.at[:, :, pl.ds(0, width)]
+
     def rs_send(k, dr, n, val, dev):
         rs_out[k, dr, n] = val.astype(BF)
-        sends.append(send(
-            rs_out.at[k, dr, n], rs_in.at[k, dr, n], rs_ssem.at[k, dr, n], rs_recv.at[k, dr, n], dev
-        ))
+        send_part(
+            lanes(rs_out.at[k, dr, n]), lanes(rs_in.at[k, dr, n]),
+            rs_ssem.at[k, dr, n], rs_recv.at[k, dr, n], dev,
+        )
 
     def reduce_first(k):
         for n, far in ((0, 1), (1, 0)):
@@ -218,7 +228,7 @@
 
     def reduce_next(k):
         for dr, (sign, dev) in enumerate(((1, zp), (-1, zm))):
-            arrived(rs_in.at[k, dr, 0], rs_recv.at[k, dr, 0])
+            part_arrived(lanes(rs_in.at[k, dr, 0]), rs_recv.at[k, dr, 0])
             rs_send(k, dr, 2, own(k, m4(z + sign), dr) + rs_in[k, dr, 0].astype(F32), dev)
 
     def chip_sum(k, q):
@@ -227,27 +237,23 @@
     def reduce_last(k):
         for n in (1, 2):
             for dr in (0, 1):
-                arrived(rs_in.at[k, dr, n], rs_recv.at[k, dr, n])
+                part_arrived(lanes(rs_in.at[k, dr, n]), rs_recv.at[k, dr, n])
         x_out[k] = chip_sum(k, 1 - xh).astype(BF)
-        sends.append(send(x_out.at[k], x_in.at[k], x_send.at[k], x_recv.at[k], xo))
-
-    def tile(k, z_, xh_, rows=16, core_=None):
-        c = core if core_ is None else core_
-        return deltas.at[
-            :,
-            pl.ds(mo(rows_of(k) + z_ * 32 + xh_ * 16, 16), rows),
-            pl.ds(mo(c * HALF, HALF), HALF),
-        ]
+        send_part(lanes(x_out.at[k]), lanes(x_in.at[k]), x_send.at[k], x_recv.at[k], xo)
+
+    def tile(k, z_, xh_, rows=16):
+        r = pl.ds(mo(rows_of(k) + z_ * 32 + xh_ * 16, 16), rows)
+        return lambda c_, width: deltas.at[:, r, pl.ds(c_ * HALF, width)]
 
     def g_out(k, n, t, rsem, dev):
-        sends.append(send(t, t, g_send.at[k, n], g_recv.at[k, rsem], dev))
+        send_part(t, t, g_send.at[k, n], g_recv.at[k, rsem], dev)
 
     def g_pair(k, n, z_):
         t = tile(k, z_, 0, 32)
-        sends.append(send(t, t, gp_send.at[k, n], gp_recv.at[k, n], pair))
+        send_part(t, t, gp_send.at[k, n], gp_recv.at[k, n], pair)
 
     def elementwise(k):
-        arrived(x_in.at[k], x_recv.at[k])
+        part_arrived(lanes(x_in.at[k]), x_recv.at[k])
         sums = chip_sum(k, xh) + x_in[k].astype(F32)
         gate, up, back = sums[0], sums[1], sums[2]
         sig = 1.0 / (1.0 + jnp.exp(-gate))
@@ -267,14 +273,14 @@
 
     def gather_x(k):
         t = tile(k, z, 1 - xh)
-        arrived(t, g_recv.at[k, 0])
+        part_arrived(t, g_recv.at[k, 0])
         g_out(k, 3, t, 1 + 1 - xh, zp)
         g_out(k, 4, t, 3 + 1 - xh, zm)
         g_pair(k, 0, z)
 
     def neighbour_tile(k, xq, n):
         for i, zz in enumerate((m4(z - 1), m4(z + 1))):
-            arrived(tile(k, zz, xq), g_recv.at[k, 1 + 2 * i + xq])
+            part_arrived(tile(k, zz, xq), g_recv.at[k, 1 + 2 * i + xq])
         src = tile(k, m4(z - 1 + 2 * xq), xq)
         dev = at(dp_=dpi(xh, m4(z + 1 - 2 * xq), core))
         g_out(k, n, src, 5 + xq, dev)
@@ -289,19 +295,21 @@
 
     def gather_far(k):
         for q in (0, 1):
-            arrived(tile(k, m4(z + 2), q), g_recv.at[k, 5 + q])
+            part_arrived(tile(k, m4(z + 2), q), g_recv.at[k, 5 + q])
         g_pair(k, 3, m4(z + 2))
 
     outs = []
 
     def backward(k):
         for n, zz in enumerate((z, m4(z - 1), m4(z + 1), m4(z + 2))):
-            arrived(tile(k, zz, 0, 32, 1 - core), gp_recv.at[k, n])
+            t = tile(k, zz, 0, 32)
+            pl.when(core == 0)(lambda: arrived(t(1, REST), gp_recv.at[k, n]))
+            pl.when(core == 1)(lambda: arrived(t(0, HALF), gp_recv.at[k, n]))
         r = pl.ds(rows_of(k), 128)
         c = pltpu.make_async_copy(deltas.at[:, r, :], deltas_out.at[:, r, :], loc_sem.at[7 + k])
         c.start()
         outs.append(c)
-        ig = contract_last(deltas[1, r, :ff], wl[0]) + contract_last(deltas[2, r, :ff], wl[1])
+        ig = dot(deltas[1, r, :ff], wl[0]) + dot(deltas[2, r, :ff], wl[1])
         if k == 0:
             ig_val[...] = ig
             ig_send[k] = ig.astype(BF)
@@ -319,28 +327,14 @@
                 ))
 
     def ready_weights():
-        their_rows = pl.ds(mo((1 - core) * d, 512), d)
-
         def settle(keep, give):
-            local_, away = down_copies(keep, give)
-            local_.wait()
-            away.wait_send()
-            arrived(wf.at[2, pl.ds(0, keep[1]), their_rows], w_recv.at[2])
-
-        @pl.when(core == 0)
-        def _():
-            settle((0, HALF), (HALF, rest))
-            for a in (0, 1):
-                pltpu.make_async_copy(*head(a, heads[a]), loc_sem.at[2 + a]).wait()
-                arrived(wf.at[a, their_rows, :], w_recv.at[a])
-                arrived(tail.at[a], w_send.at[a])
-
-        @pl.when(core == 1)
-        def _():
-            settle((HALF, rest), (0, HALF))
-            for a in (0, 1):
-                arrived(wf.at[a, their_rows, pl.ds(0, TAIL)], w_recv.at[a])
-                arrived(wf.at[a, my_rows, :], w_send.at[a])
+            for a in range(3):
+                local_, away = weight_copies(a, keep, give)
+                local_.wait()
+                away.wait_send()
+                arrived(wf.at[a, pl.ds(0, keep[1]), their_rows], w_recv.at[a])
+
+        on_core(settle)
 
     from_neighbours(xl, 1, 2, 5)
     ready_weights()
@@ -358,6 +352,8 @@
     forward(3)
     reduce_first(3)
     reduce_last(0)
+    for c in full:
+        c.wait()
     c = pltpu.make_async_copy(xin.at[:, :, pl.ds(mo(core * d, 512), d)], rows_out, loc_sem.at[11])
     c.start()
     outs.append(c)
@@ -385,6 +381,8 @@
     ig_out[...] = total.astype(BF)
     for c in sends:
         c.wait_send()
+    for copy in part_sends:
+        each_width(lambda c_, width: copy(c_, width).wait_send())
     for c in outs:
         c.wait()
 
@@ -406,13 +404,12 @@
         scratch_shapes=[
             pltpu.VMEM((2, 512, 2 * d), BF),
             pltpu.VMEM((3, HALF, HALF), BF),
-            pltpu.VMEM((2, d, gate_w.shape[1]), BF),
+            pltpu.VMEM((2, gate_w.shape[0], d), BF),
             pltpu.VMEM((4, 3, 128, HALF), F32),
             pltpu.VMEM((4, 2, 3, 3, 16, HALF), BF),
             pltpu.VMEM((4, 2, 3, 3, 16, HALF), BF),
             pltpu.VMEM((4, 3, 16, HALF), BF),
             pltpu.VMEM((4, 3, 16, HALF), BF),
-            pltpu.VMEM((2, d, TAIL), BF),
             pltpu.VMEM((3, 512, 2 * HALF), BF),
             pltpu.VMEM((8, 64, d), BF),
             pltpu.VMEM((4, 128, d), BF),
@@ -430,8 +427,8 @@
 
 
 def grads_kernel(rows, deltas, gate_ref, up_ref, down_ref):
-    gate_ref[...] = contract_first(rows[0], deltas[1]).astype(BF)
-    up_ref[...] = contract_first(rows[0], deltas[2]).astype(BF)
+    gate_ref[...] = contract_first(deltas[1], rows[0]).astype(BF)
+    up_ref[...] = contract_first(deltas[2], rows[0]).astype(BF)
     down_ref[...] = contract_first(deltas[0], rows[1]).astype(BF)
 
 
@@ -442,28 +439,20 @@
         grads_kernel,
         name="weight_grads",
         grid=(pl.cdiv(ff, n),),
-        out_shape=(
-            jax.ShapeDtypeStruct((d, ff), BF),
-            jax.ShapeDtypeStruct((d, ff), BF),
-            jax.ShapeDtypeStruct((ff, d), BF),
-        ),
+        out_shape=(jax.ShapeDtypeStruct((ff, d), BF),) * 3,
         in_specs=[
             pl.BlockSpec((2, 512, d), lambda i: (0, 0, 0)),
             pl.BlockSpec((3, 512, n), lambda i: (0, 0, i)),
         ],
-        out_specs=(
-            pl.BlockSpec((d, n), lambda i: (0, i)),
-            pl.BlockSpec((d, n), lambda i: (0, i)),
-            pl.BlockSpec((n, d), lambda i: (i, 0)),
-        ),
-        compiler_params=pltpu.CompilerParams(vmem_limit_bytes=40 * 1024 * 1024),
+        out_specs=(pl.BlockSpec((n, d), lambda i: (i, 0)),) * 3,
+        compiler_params=pltpu.CompilerParams(vmem_limit_bytes=62 * 1024 * 1024),
     )(rows, deltas)
 
 
 def local(inputs, upstream, gate_weight, up_weight, down_weight):
-    input_grad, deltas, rows = fused(inputs, upstream, gate_weight, up_weight, down_weight)
-    gate_grad, up_grad, down_grad = weight_grads(rows, deltas, gate_weight.shape[1])
-    return (input_grad, gate_grad, up_grad, down_grad)
+    input_grad, deltas, rows = fused(inputs, upstream, gate_weight.T, up_weight.T, down_weight)
+    gate_grad, up_grad, down_grad = weight_grads(rows, deltas, down_weight.shape[0])
+    return (input_grad, gate_grad.T, up_grad.T, down_grad)
 
 
 def solution(mesh):

time: 105 us -> 86.4 us (0.82)
  local copies, waits for them, and re-layouts: 18.8 us -> 0.63 us
    unnamed x15 -> x3, local copies, waits for them, and re-layouts: 18.8 us -> 0.63 us
    pallas_call x1, Pallas kernels: 79.2 us -> 77.1 us  [fused(): pl.pallas_call(kernel, name='fused', out_shape=(jax.ShapeDtypeStruct((64,...]
    pallas_call x1, Pallas kernels: 5.8 us -> 7.87 us  [weight_grads(): pl.pallas_call(grads_kernel, name='weight_grads', grid=(pl.cdiv(ff, n),),...]
where the time goes in v3:
time: 86.4 us; the launch traced here: 86.3 us
  Pallas kernels  85 us (98%)
    pallas_call x1, Pallas kernels, fused(): pl.pallas_call(kernel, name='fused', out_shape=(jax.ShapeDtypeStruct((64,...  77.1 us
    pallas_call x1, Pallas kernels, weight_grads(): pl.pallas_call(grads_kernel, name='weight_grads', grid=(pl.cdiv(ff, n),),...  7.87 us

profile of v3, /device:TPU:1, one launch (start us, length us, event | category | flops | bytes accessed | tf_op | source)
XLA Modules:
  0.0 86.3 jit_solution(8586770158799317322)
XLA Ops:
  0.6 77.1 %fused.1 = (bf16[64,512]{1,0:T(8,128)(2,1)}, bf16[3,512,2048]{2,1,0:T(8,128)(2,1)}, bf16[2,512,512]{2,1,0:T(8,128)(2,1)}) custom-call(bf16[64,512]{1,0:T(8,128)(2,1)} %inputs.1, bf16[64,512]{1,0:T(8,128)(2,1)} %upstream.1, bf16[1848,512]{1,0:T(8,128)(2,1)} %bitcast.4, bf16[1848,512]{1,0:T(8,128)(2,1)} %bitcast.5, bf16[1848,512]{1,0:T(8,128)(2,1)} %down_w.1), custom_call_target="tpu_custom_call" | custom-call | flops 5000000000 | bytes 20000000 | tf_op jit(solution)/shard_map/fused/pallas_call | solution.py:394
  77.7 0.0 copy-start
  77.7 7.9 %weight_grads.1 = (bf16[1848,512]{1,0:T(8,128)(2,1)}, bf16[1848,512]{1,0:T(8,128)(2,1)}, bf16[1848,512]{1,0:T(8,128)(2,1)}) custom-call(bf16[2,512,512]{2,1,0:T(8,128)(2,1)} %get-tuple-element.11.rows, bf16[3,512,2048]{2,1,0:T(8,128)(2,1)} %get-tuple-element.12.deltas), custom_call_target="tpu_custom_call" | custom-call | tf_op jit(solution)/shard_map/weight_grads/pallas_call | solution.py:438
  85.6 0.0 copy-done
  85.6 0.6 copy.10
Async XLA Ops:
  77.7 7.9 %copy-start = (bf16[64,512]{1,0:T(8,128)(2,1)S(1)}, bf16[64,512]{1,0:T(8,128)(2,1)}, u32[]{:S(2)}) copy-start(bf16[64,512]{1,0:T(8,128)(2,1)} %get-tuple-element.20) | copy-start | bytes 196612
